TPU v7x, 32 devices: a whole 2x2x4 slice. The times are simulated.
32 devices in a mesh: dp: 4 (over y, x), centers: 8 (over z, core).
Axes of the slice: x: 2, y: 2, z: 4, core: 2. Of those that a mesh axis runs over, the one named last changes fastest.
Arguments:
- points: bfloat16 [16384, 32], P('dp'), may hold values from -6 to 6
- centers: bfloat16 [16384, 32], P('centers'), may hold values from -6 to 6
- coef: bfloat16 [16384, 64], P('centers'), may hold values from -0.1875 to 0.1875
Outputs:
- product: float32 [16384, 64], P('centers')
All inputs are finite; a program needn't handle non-finite values.
Results may differ from a plain program's by a relative error of at most 0.0003.
Values may be sent and summed in bfloat16 or wider, within the bound.
No kernel may reach another device: no remote copies, remote signals or barrier semaphores. Data moves between devices by JAX's collectives and lax.ppermute only.
A program may use at most 128 MiB of HBM per device.

v0:
```python
import jax
import jax.numpy as jnp
from jax import lax
from jax.sharding import PartitionSpec as P


def kernel_block(left_pts, left_sq, right_pts, right_sq, features):
    inner = lax.dot_general(
        left_pts, right_pts, (((1,), (1,)), ((), ())), preferred_element_type=jnp.float32
    )
    dist = left_sq[:, None] + right_sq[None, :] - 2.0 * inner
    return jnp.exp(dist * (-2.0 / features)).astype(jnp.bfloat16)


def squares(values):
    wide = values.astype(jnp.float32)
    return jnp.sum(wide * wide, axis=1)


def on_device(points, centers, coef):
    features = points.shape[1]
    local_pts = points.shape[0]
    local_cen = centers.shape[0]
    outs_count = coef.shape[1]
    block_pts = min(1024, local_pts)
    block_count = local_pts // block_pts
    cen_sq = squares(centers)
    point_blocks = points.reshape(block_count, block_pts, features)
    scalar_zero = jnp.zeros((), jnp.float32)

    def forward_keep(carry, block):
        kernel = kernel_block(block, squares(block), centers, cen_sq, features)
        return (carry, (kernel, jnp.dot(kernel, coef, preferred_element_type=jnp.float32)))

    unused, (tiles, partial_value) = lax.scan(forward_keep, scalar_zero, point_blocks)
    forward_part = partial_value.reshape(local_pts, outs_count)
    shared = lax.psum_scatter(
        forward_part.astype(jnp.bfloat16), "centers", scatter_dimension=0, tiled=True
    )
    forward = lax.all_gather(shared, "centers", axis=0, tiled=True)
    forward_blocks = forward.reshape(block_count, block_pts, outs_count)
    back = jnp.einsum("bij,bio->jo", tiles, forward_blocks, preferred_element_type=jnp.float32)
    total_pts = local_pts * lax.axis_size("dp")
    back = back * (1.0 / jnp.sqrt(jnp.float32(total_pts)))
    own_count = local_cen // lax.axis_size("dp")
    own_start = lax.axis_index("dp") * own_count
    own_cen = lax.dynamic_slice_in_dim(centers, own_start, own_count, 0)
    own_sq = squares(own_cen)
    piece_cen = lax.all_gather(centers, "centers", axis=0, tiled=True)
    piece_coef = lax.all_gather(coef, "centers", axis=0, tiled=True)
    kernel = kernel_block(own_cen, own_sq, piece_cen, squares(piece_cen), features)
    regular = jnp.dot(kernel, piece_coef, preferred_element_type=jnp.float32)
    placed = lax.dynamic_update_slice_in_dim(jnp.zeros_like(back), regular, own_start, 0)
    return lax.psum(back + placed, "dp")


def solution(mesh):
    in_specs = (P("dp", None), P("centers", None), P("centers", None))
    out_specs = P("centers", None)
    return jax.shard_map(
        on_device, mesh=mesh, in_specs=in_specs, out_specs=out_specs, check_vma=False
    )
```

profile of v0, /device:TPU:0, one launch (start us, length us, event | category | flops | bytes accessed | tf_op | source)
XLA Modules:
  0.0 192.9 jit_solution(11572367523075643524)
XLA Ops:
  6.5 1.4 copy.5
  8.0 1.0 multiply_reduce_fusion.2
  8.9 27.9 %while.12 = (s32[]{:T(128)}, bf16[4,1024,2048]{2,1,0:T(8,128)(2,1)}, bf16[4,1024,64]{1,2,0:T(8,128)(2,1)S(1)}, bf16[4,1024,32]{2,1,0:T(8,128)(2,1)S(1)}, f32[204...) while((s32[]{:T(128)}, bf16[4,1024,2048]{2,1,0:T(8,128)(2,1)}, ...), condition=%wide.region_3.4_spmd, body=%wide.region_1.3_spmd.sunk | while | flops 413236224 | bytes 13583461 | solution.py:35
  8.9 0.2 multiply_reduce_fusion.5
  9.2 4.4 %bitcast_dynamic-update-slice_fusion.2 = (bf16[4,1024,2048]{2,1,0:T(8,128)(2,1)}, bf16[1024,2048]{1,0:T(8,128)(2,1)S(1)}) fusion(bf16[4,1024,2048]{2,1,0:T(8,128)(2,1)} %get-tuple-element.117, s32[]{:T(128)S(6)} %copy.19, bf16[2048,32]{0,1:T(8,128)(2,1)} %get-tuple-element.129, bf16[4,1024,32]{2,1,0:T(8,128)(2,1)S(1)} %get-tuple-element.127, ...), kind=kOutput, calls=%fused_computation.1.clone.1 | convolution fusion | flops 144703488 | bytes 8795136 | tf_op jit(solution)/shard_map/while/body/eval_jaxpr/dot_general | solution.py:8
  13.5 2.3 %fusion.29 = bf16[4,1024,64]{1,2,0:T(8,128)(2,1)S(1)} fusion(bf16[4,1024,64]{1,2,0:T(8,128)(2,1)S(1)} %get-tuple-element.118, s32[]{:T(128)S(6)} %copy.19, bf16[1024,2048]{1,0:T(8,128)(2,1)S(1)} %get-tuple-element.107, bf16[2048,64]{0,1:T(8,128)(2,1)} %get-tuple-element.130), kind=kOutput, calls=%fused_computation.3.clone.1 | convolution fusion | flops 268435456 | bytes 4718596 | tf_op jit(solution)/shard_map/while/body/eval_jaxpr/dot_general | solution.py:33
  15.9 0.2 multiply_reduce_fusion.5
  16.1 4.4 %bitcast_dynamic-update-slice_fusion.2 = (bf16[4,1024,2048]{2,1,0:T(8,128)(2,1)}, bf16[1024,2048]{1,0:T(8,128)(2,1)S(1)}) fusion(bf16[4,1024,2048]{2,1,0:T(8,128)(2,1)} %get-tuple-element.117, s32[]{:T(128)S(6)} %copy.19, bf16[2048,32]{0,1:T(8,128)(2,1)} %get-tuple-element.129, bf16[4,1024,32]{2,1,0:T(8,128)(2,1)S(1)} %get-tuple-element.127, ...), kind=kOutput, calls=%fused_computation.1.clone.1 | convolution fusion | flops 144703488 | bytes 8795136 | tf_op jit(solution)/shard_map/while/body/eval_jaxpr/dot_general | solution.py:8
  20.5 2.3 %fusion.29 = bf16[4,1024,64]{1,2,0:T(8,128)(2,1)S(1)} fusion(bf16[4,1024,64]{1,2,0:T(8,128)(2,1)S(1)} %get-tuple-element.118, s32[]{:T(128)S(6)} %copy.19, bf16[1024,2048]{1,0:T(8,128)(2,1)S(1)} %get-tuple-element.107, bf16[2048,64]{0,1:T(8,128)(2,1)} %get-tuple-element.130), kind=kOutput, calls=%fused_computation.3.clone.1 | convolution fusion | flops 268435456 | bytes 4718596 | tf_op jit(solution)/shard_map/while/body/eval_jaxpr/dot_general | solution.py:33
  22.9 0.2 multiply_reduce_fusion.5
  23.1 4.4 %bitcast_dynamic-update-slice_fusion.2 = (bf16[4,1024,2048]{2,1,0:T(8,128)(2,1)}, bf16[1024,2048]{1,0:T(8,128)(2,1)S(1)}) fusion(bf16[4,1024,2048]{2,1,0:T(8,128)(2,1)} %get-tuple-element.117, s32[]{:T(128)S(6)} %copy.19, bf16[2048,32]{0,1:T(8,128)(2,1)} %get-tuple-element.129, bf16[4,1024,32]{2,1,0:T(8,128)(2,1)S(1)} %get-tuple-element.127, ...), kind=kOutput, calls=%fused_computation.1.clone.1 | convolution fusion | flops 144703488 | bytes 8795136 | tf_op jit(solution)/shard_map/while/body/eval_jaxpr/dot_general | solution.py:8
  27.5 2.3 %fusion.29 = bf16[4,1024,64]{1,2,0:T(8,128)(2,1)S(1)} fusion(bf16[4,1024,64]{1,2,0:T(8,128)(2,1)S(1)} %get-tuple-element.118, s32[]{:T(128)S(6)} %copy.19, bf16[1024,2048]{1,0:T(8,128)(2,1)S(1)} %get-tuple-element.107, bf16[2048,64]{0,1:T(8,128)(2,1)} %get-tuple-element.130), kind=kOutput, calls=%fused_computation.3.clone.1 | convolution fusion | flops 268435456 | bytes 4718596 | tf_op jit(solution)/shard_map/while/body/eval_jaxpr/dot_general | solution.py:33
  29.8 0.2 multiply_reduce_fusion.5
  30.1 4.4 %bitcast_dynamic-update-slice_fusion.2 = (bf16[4,1024,2048]{2,1,0:T(8,128)(2,1)}, bf16[1024,2048]{1,0:T(8,128)(2,1)S(1)}) fusion(bf16[4,1024,2048]{2,1,0:T(8,128)(2,1)} %get-tuple-element.117, s32[]{:T(128)S(6)} %copy.19, bf16[2048,32]{0,1:T(8,128)(2,1)} %get-tuple-element.129, bf16[4,1024,32]{2,1,0:T(8,128)(2,1)S(1)} %get-tuple-element.127, ...), kind=kOutput, calls=%fused_computation.1.clone.1 | convolution fusion | flops 144703488 | bytes 8795136 | tf_op jit(solution)/shard_map/while/body/eval_jaxpr/dot_general | solution.py:8
  34.5 2.3 %fusion.29 = bf16[4,1024,64]{1,2,0:T(8,128)(2,1)S(1)} fusion(bf16[4,1024,64]{1,2,0:T(8,128)(2,1)S(1)} %get-tuple-element.118, s32[]{:T(128)S(6)} %copy.19, bf16[1024,2048]{1,0:T(8,128)(2,1)S(1)} %get-tuple-element.107, bf16[2048,64]{0,1:T(8,128)(2,1)} %get-tuple-element.130), kind=kOutput, calls=%fused_computation.3.clone.1 | convolution fusion | flops 268435456 | bytes 4718596 | tf_op jit(solution)/shard_map/while/body/eval_jaxpr/dot_general | solution.py:33
  36.8 0.8 copy.9
  37.7 0.0 all-gather.3.cloned.1.call-start
  37.7 0.7 all-gather.3.cloned.1.call-update
  38.4 0.0 all-gather.5.cloned.1.call-start
  38.5 0.7 all-gather.5.cloned.1.call-update
  39.2 0.0 all-reduce.2.cloned.1.call-start
  39.2 0.8 multiply_reduce_fusion.3
  40.0 31.9 %reduce-scatter.2.cloned.1.call-done = bf16[512,64]{0,1:T(8,128)(2,1)} async-done(((bf16[4096,64]{0,1:T(8,128)(2,1)}), bf16[512,64]{0,1:T(8,128)(2,1)}) %reduce-scatter.2.cloned.1.call-update) | async-done | bytes 65552 | tf_op jit(solution)/shard_map/reduce_scatter | solution.py:37
  71.9 16.8 %all_gather.9 = bf16[4096,64]{0,1:T(8,128)(2,1)S(1)} all-gather(bf16[512,64]{0,1:T(8,128)(2,1)} %reduce-scatter.2.cloned.1.call-done), channel_id=1, replica_groups=mesh['dp'=4,'centers'=8] {'centers'}, dimensions={0}, use_global_device_ids=true | all-gather | bytes 589824 | tf_op jit(solution)/shard_map/all_gather | solution.py:40
  88.7 8.9 %fusion.5 = f32[2048,64]{0,1:T(8,128)S(1)} fusion(bf16[4,1024,2048]{2,1,0:T(8,128)(2,1)} %get-tuple-element.43, bf16[8,4,8,1024]{3,2,1,0:T(8,128)(2,1)S(1)} %bitcast.46), kind=kOutput, calls=%fused_computation.11 | convolution fusion | flops 1073872896 | bytes 17825792 | tf_op jit(solution)/shard_map/bij,bio->jo/dot_general | solution.py:42
  97.6 0.0 all-gather.3.cloned.1.call-done
  97.6 1.5 multiply_reduce_fusion.1
  99.2 26.4 %all-gather.5.cloned.1.call-done = bf16[16384,64]{0,1:T(8,128)(2,1)} async-done(((bf16[2048,64]{0,1:T(8,128)(2,1)}), bf16[16384,64]{0,1:T(8,128)(2,1)}) %all-gather.5.cloned.1.call-update) | async-done | bytes 2097168 | tf_op jit(solution)/shard_map/all_gather | solution.py:50
  125.6 13.2 %fusion.7 = f32[2048,64]{0,1:T(8,128)S(1)} fusion(f32[2048,64]{0,1:T(8,128)S(1)} %fusion.5, s32[]{:T(128)S(6)} %select_n.4, bf16[16384,64]{0,1:T(8,128)(2,1)} %all-gather.5.cloned.1.call-done, bf16[16384,32]{0,1:T(8,128)(2,1)} %all-gather.3.cloned.1.call-done, f32[16384]{0:T(1024)S(1)} %multiply_reduce_fusion.1, f32[512]{0:T(512)S(1)} %multiply_reduce_fusion.3, ...), kind=kOutput, calls=%fused_computation.14 | convolution fusion | flops 1652588544 | bytes 3509248 | tf_op jit(solution)/shard_map/dot_general | solution.py:52
  138.8 0.8 copy-done
  139.6 44.9 %all-reduce.2.cloned.1.call-done = f32[2048,64]{0,1:T(8,128)} async-done(((f32[2048,64]{0,1:T(8,128)}), f32[2048,64]{0,1:T(8,128)}) %all-reduce.2.cloned.1.call-update) | async-done | bytes 524304 | tf_op jit(solution)/shard_map/psum | solution.py:54
  184.5 1.9 copy.27
  (6 shorter events, 0.0 us)
Async XLA Ops:
  6.5 65.4 %reduce-scatter.2.cloned.1.call-start = ((), (), s32[]{:S(2)}) async-start(), calls=%async_computation.1 | async-start | bytes 589824 | tf_op jit(solution)/shard_map/reduce_scatter | solution.py:37
  37.7 59.9 %all-gather.3.cloned.1.call-start = ((), (), s32[]{:S(2)}) async-start(), calls=%async_computation.2 | async-start | bytes 1179648 | tf_op jit(solution)/shard_map/all_gather | solution.py:49
  38.4 87.2 %all-gather.5.cloned.1.call-start = ((), (), s32[]{:S(2)}) async-start(), calls=%async_computation.3 | async-start | bytes 2359296 | tf_op jit(solution)/shard_map/all_gather | solution.py:50
  39.2 145.4 %all-reduce.2.cloned.1.call-start = ((), (), s32[]{:S(2)}) async-start(), calls=%async_computation.4 | async-start | bytes 1048576 | tf_op jit(solution)/shard_map/psum | solution.py:54
  138.8 0.8 copy-start
Sparse Core Ops, SparseCore 0:
  37.8 34.0 reduce-scatter.1
  73.5 21.7 all-gather.2
  96.9 28.6 all-gather.4
  139.7 44.7 all-reduce.1
where the time goes:
time: 193 us
  waiting for transfers between devices  105 us (54%)
  matrix products  49 us (25%)
  blocking collectives  16.8 us (9%)
  between operations  13.2 us (7%)
  local copies, waits for them, and re-layouts  4.92 us (3%)
  other arithmetic  4.13 us (2%)
    psum x1, waiting for transfers between devices, on_device(): return lax.psum(back + placed, 'dp')  44.9 us
    reduce_scatter x1, waiting for transfers between devices, on_device(): lax.psum_scatter(forward_part.astype(jnp.bfloat16), 'centers', scatter_di...  31.9 us
    all_gather x1, waiting for transfers between devices, on_device(): piece_coef = lax.all_gather(coef, 'centers', axis=0, tiled=True)  26.4 us
    dot_general x4, matrix products, kernel_block(): lax.dot_general(left_pts, right_pts, (((1,), (1,)), ((), ())), preferred_...  17.6 us
    all_gather x1, blocking collectives, on_device(): forward = lax.all_gather(shared, 'centers', axis=0, tiled=True)  16.8 us
    dot_general x1, matrix products, on_device(): regular = jnp.dot(kernel, piece_coef, preferred_element_type=jnp.float32)  13.2 us
    dot_general x4, matrix products, forward_keep(): jnp.dot(kernel, coef, preferred_element_type=jnp.float32)  9.35 us
    dot_general x1, matrix products, on_device(): jnp.einsum('bij,bio->jo', tiles, forward_blocks, preferred_element_type=j...  8.89 us
  transfers between devices with their start and end apart: 4, of which 3 were waited for; matrix products, arithmetic and copies ran while one was open for 6% of the time, Pallas kernels for 0%

commit v1 on v0

--- a/solution.py
+++ b/solution.py
@@ -47,7 +47,14 @@
     own_cen = lax.dynamic_slice_in_dim(centers, own_start, own_count, 0)
     own_sq = squares(own_cen)
     piece_cen = lax.all_gather(centers, "centers", axis=0, tiled=True)
-    piece_coef = lax.all_gather(coef, "centers", axis=0, tiled=True)
+    ring = [coef]
+    for hop in range(7):
+        ring.append(lax.ppermute(ring[-1], "centers", [(dev, (dev + 1) % 8) for dev in range(8)]))
+    piece_coef = jnp.roll(
+        jnp.concatenate(ring[::-1], axis=0),
+        (lax.axis_index("centers") + 1) * ring[0].shape[0],
+        axis=0,
+    )
     kernel = kernel_block(own_cen, own_sq, piece_cen, squares(piece_cen), features)
     regular = jnp.dot(kernel, piece_coef, preferred_element_type=jnp.float32)
     placed = lax.dynamic_update_slice_in_dim(jnp.zeros_like(back), regular, own_start, 0)

time: 193 us -> 181 us (0.938)
  waiting for transfers between devices: 105 us -> 84.3 us
  local copies, waits for them, and re-layouts: 4.92 us -> 16.5 us
  matrix products: 49 us -> 45.4 us
    ppermute x0 -> x7, waiting for transfers between devices: none -> 29.5 us  [on_device(): lax.ppermute(ring[-1], 'centers', [(dev, (dev + 1) % 8) for dev in range(...]
    all_gather x1 -> x0, waiting for transfers between devices: 26.4 us -> none  [on_device(): piece_coef = lax.all_gather(coef, 'centers', axis=0, tiled=True)]
    reduce_scatter x1, waiting for transfers between devices: 31.9 us -> 8.35 us  [on_device(): lax.psum_scatter(forward_part.astype(jnp.bfloat16), 'centers', scatter_di...]
    unnamed x4 -> x21, local copies, waits for them, and re-layouts: 4.08 us -> 14.9 us
    dot_general x4, matrix products: 9.35 us -> 5.56 us  [forward_keep(): jnp.dot(kernel, coef, preferred_element_type=jnp.float32)]
  transfers between devices with their start and end apart: 4 -> 10, of which waited for: 3 -> 6; matrix products, arithmetic and copies ran while one was open for 6% -> 27% of each run, Pallas kernels for 0% -> 0%
where the time goes in v1:
time: 181 us
  waiting for transfers between devices  84.3 us (47%)
  matrix products  45.4 us (25%)
  local copies, waits for them, and re-layouts  16.5 us (9%)
  blocking collectives  15.9 us (9%)
  between operations  13.2 us (7%)
  other arithmetic  4.13 us (2%)
    psum x1, waiting for transfers between devices, on_device(): return lax.psum(back + placed, 'dp')  46.4 us
    ppermute x7, waiting for transfers between devices, on_device(): lax.ppermute(ring[-1], 'centers', [(dev, (dev + 1) % 8) for dev in range(...  29.5 us
    dot_general x4, matrix products, kernel_block(): lax.dot_general(left_pts, right_pts, (((1,), (1,)), ((), ())), preferred_...  17.8 us
    all_gather x1, blocking collectives, on_device(): forward = lax.all_gather(shared, 'centers', axis=0, tiled=True)  15.9 us
    unnamed x21, local copies, waits for them, and re-layouts  14.9 us
    dot_general x1, matrix products, on_device(): regular = jnp.dot(kernel, piece_coef, preferred_element_type=jnp.float32)  13.2 us
    dot_general x1, matrix products, on_device(): jnp.einsum('bij,bio->jo', tiles, forward_blocks, preferred_element_type=j...  8.95 us
    reduce_scatter x1, waiting for transfers between devices, on_device(): lax.psum_scatter(forward_part.astype(jnp.bfloat16), 'centers', scatter_di...  8.35 us
  transfers between devices with their start and end apart: 10, of which 6 were waited for; matrix products, arithmetic and copies ran while one was open for 27% of the time, Pallas kernels for 0%

profile of v1, /device:TPU:0, one launch (start us, length us, event | category | flops | bytes accessed | tf_op | source)
XLA Modules:
  0.0 180.9 jit_solution(2198921239967663574)
XLA Ops:
  7.0 1.4 copy.5
  8.5 1.0 multiply_reduce_fusion.2
  9.4 5.9 %collective-permute-done = bf16[2048,64]{0,1:T(8,128)(2,1)S(1)} collective-permute-done((bf16[2048,64]{0,1:T(8,128)(2,1)}, bf16[2048,64]{0,1:T(8,128)(2,1)S(1)}, u32[]{:S(2)}, u32[]{:S(2)}) %collective-permute-start) | collective-permute-done | bytes 262176 | tf_op jit(solution)/shard_map/ppermute | solution.py:52
  15.3 24.3 %while.12 = (s32[]{:T(128)}, bf16[4,1024,2048]{2,1,0:T(8,128)(2,1)}, bf16[4,1024,64]{1,2,0:T(8,128)(2,1)S(1)}, bf16[4,1024,32]{2,1,0:T(8,128)(2,1)S(1)}, f32[204...) while((s32[]{:T(128)}, bf16[4,1024,2048]{2,1,0:T(8,128)(2,1)}, ...), condition=%wide.region_3.4_spmd, body=%wide.region_1.3_spmd.sunk | while | flops 413236224 | bytes 14632065 | solution.py:35
  15.6 4.4 %bitcast_dynamic-update-slice_fusion.2 = (bf16[4,1024,2048]{2,1,0:T(8,128)(2,1)}, bf16[1024,2048]{1,0:T(8,128)(2,1)S(1)}) fusion(bf16[4,1024,2048]{2,1,0:T(8,128)(2,1)} %get-tuple-element.117, s32[]{:T(128)S(6)} %copy.19, bf16[2048,32]{0,1:T(8,128)(2,1)} %get-tuple-element.129, bf16[4,1024,32]{2,1,0:T(8,128)(2,1)S(1)} %get-tuple-element.127, ...), kind=kOutput, calls=%fused_computation.1.clone.1 | convolution fusion | flops 144703488 | bytes 8795136 | tf_op jit(solution)/shard_map/while/body/eval_jaxpr/dot_general | solution.py:8
  20.0 1.4 fusion.33
  21.6 4.5 %bitcast_dynamic-update-slice_fusion.2 = (bf16[4,1024,2048]{2,1,0:T(8,128)(2,1)}, bf16[1024,2048]{1,0:T(8,128)(2,1)S(1)}) fusion(bf16[4,1024,2048]{2,1,0:T(8,128)(2,1)} %get-tuple-element.117, s32[]{:T(128)S(6)} %copy.19, bf16[2048,32]{0,1:T(8,128)(2,1)} %get-tuple-element.129, bf16[4,1024,32]{2,1,0:T(8,128)(2,1)S(1)} %get-tuple-element.127, ...), kind=kOutput, calls=%fused_computation.1.clone.1 | convolution fusion | flops 144703488 | bytes 8795136 | tf_op jit(solution)/shard_map/while/body/eval_jaxpr/dot_general | solution.py:8
  26.1 1.4 fusion.33
  27.7 4.4 %bitcast_dynamic-update-slice_fusion.2 = (bf16[4,1024,2048]{2,1,0:T(8,128)(2,1)}, bf16[1024,2048]{1,0:T(8,128)(2,1)S(1)}) fusion(bf16[4,1024,2048]{2,1,0:T(8,128)(2,1)} %get-tuple-element.117, s32[]{:T(128)S(6)} %copy.19, bf16[2048,32]{0,1:T(8,128)(2,1)} %get-tuple-element.129, bf16[4,1024,32]{2,1,0:T(8,128)(2,1)S(1)} %get-tuple-element.127, ...), kind=kOutput, calls=%fused_computation.1.clone.1 | convolution fusion | flops 144703488 | bytes 8795136 | tf_op jit(solution)/shard_map/while/body/eval_jaxpr/dot_general | solution.py:8
  32.2 1.4 fusion.33
  33.8 4.4 %bitcast_dynamic-update-slice_fusion.2 = (bf16[4,1024,2048]{2,1,0:T(8,128)(2,1)}, bf16[1024,2048]{1,0:T(8,128)(2,1)S(1)}) fusion(bf16[4,1024,2048]{2,1,0:T(8,128)(2,1)} %get-tuple-element.117, s32[]{:T(128)S(6)} %copy.19, bf16[2048,32]{0,1:T(8,128)(2,1)} %get-tuple-element.129, bf16[4,1024,32]{2,1,0:T(8,128)(2,1)S(1)} %get-tuple-element.127, ...), kind=kOutput, calls=%fused_computation.1.clone.1 | convolution fusion | flops 144703488 | bytes 8795136 | tf_op jit(solution)/shard_map/while/body/eval_jaxpr/dot_general | solution.py:8
  38.2 1.4 fusion.33
  39.6 0.8 copy.9
  41.0 7.2 %collective-permute-done.2 = bf16[2048,64]{0,1:T(8,128)(2,1)S(1)} collective-permute-done((bf16[2048,64]{0,1:T(8,128)(2,1)S(1)}, bf16[2048,64]{0,1:T(8,128)(2,1)S(1)}, u32[]{:S(2)}, u32[]{:S(2)}) %collective-permute-start.2) | collective-permute-done | bytes 262176 | tf_op jit(solution)/shard_map/ppermute | solution.py:52
  48.2 8.3 %collective-permute-done.3 = bf16[2048,64]{0,1:T(8,128)(2,1)S(1)} collective-permute-done((bf16[2048,64]{0,1:T(8,128)(2,1)S(1)}, bf16[2048,64]{0,1:T(8,128)(2,1)S(1)}, u32[]{:S(2)}, u32[]{:S(2)}) %collective-permute-start.3) | collective-permute-done | bytes 262176 | tf_op jit(solution)/shard_map/ppermute | solution.py:52
  56.5 8.1 %collective-permute-done.4 = bf16[2048,64]{0,1:T(8,128)(2,1)S(1)} collective-permute-done((bf16[2048,64]{0,1:T(8,128)(2,1)S(1)}, bf16[2048,64]{0,1:T(8,128)(2,1)S(1)}, u32[]{:S(2)}, u32[]{:S(2)}) %collective-permute-start.4) | collective-permute-done | bytes 262176 | tf_op jit(solution)/shard_map/ppermute | solution.py:52
  64.7 0.8 multiply_reduce_fusion.3
  65.5 8.4 %reduce-scatter.2.cloned.1.call-done = bf16[512,64]{0,1:T(8,128)(2,1)} async-done(((bf16[4096,64]{0,1:T(8,128)(2,1)}), bf16[512,64]{0,1:T(8,128)(2,1)}) %reduce-scatter.2.cloned.1.call-update) | async-done | bytes 65552 | tf_op jit(solution)/shard_map/reduce_scatter | solution.py:37
  73.8 15.9 %all_gather.6 = bf16[4096,64]{0,1:T(8,128)(2,1)S(1)} all-gather(bf16[512,64]{0,1:T(8,128)(2,1)} %reduce-scatter.2.cloned.1.call-done), channel_id=1, replica_groups=mesh['dp'=4,'centers'=8] {'centers'}, dimensions={0}, use_global_device_ids=true | all-gather | bytes 589824 | tf_op jit(solution)/shard_map/all_gather | solution.py:40
  90.1 8.9 %fusion.5 = f32[2048,64]{0,1:T(8,128)S(1)} fusion(bf16[4,1024,2048]{2,1,0:T(8,128)(2,1)} %get-tuple-element.43, bf16[8,4,8,1024]{3,2,1,0:T(8,128)(2,1)S(1)} %bitcast.45), kind=kOutput, calls=%fused_computation.11 | convolution fusion | flops 1073872896 | bytes 17825792 | tf_op jit(solution)/shard_map/bij,bio->jo/dot_general | solution.py:42
  102.6 0.7 constant_dynamic-update-slice_fusion.10
  103.3 0.7 constant_dynamic-update-slice_fusion.9
  104.8 0.7 constant_dynamic-update-slice_fusion.7
  105.5 0.7 constant_dynamic-update-slice_fusion.6
  107.7 0.8 constant_dynamic-update-slice_fusion.3
  109.1 0.7 constant_dynamic-update-slice_fusion.1
  109.8 0.7 constant_dynamic-update-slice_fusion
  110.6 1.5 multiply_reduce_fusion.1
  112.1 13.2 %fusion.10 = f32[2048,64]{0,1:T(8,128)S(1)} fusion(f32[2048,64]{0,1:T(8,128)S(1)} %fusion.5, s32[]{:T(128)S(6)} %select_n.17, bf16[32768,64]{0,1:T(8,128)(2,1)} %constant_dynamic-update-slice_fusion, s32[]{:T(128)S(6)} %select_n.19, bf16[16384,32]{0,1:T(8,128)(2,1)} %all-gather.2.cloned.1.call-done, f32[16384]{0:T(1024)S(1)} %multiply_reduce_fusion.1, ...), kind=kOutput, calls=%fused_computation.15 | convolution fusion | flops 1652588544 | bytes 3509760 | tf_op jit(solution)/shard_map/dot_general | solution.py:59
  125.3 0.8 copy-done.2
  126.1 46.4 %all-reduce.2.cloned.1.call-done = f32[2048,64]{0,1:T(8,128)} async-done(((f32[2048,64]{0,1:T(8,128)}), f32[2048,64]{0,1:T(8,128)}) %all-reduce.2.cloned.1.call-update) | async-done | bytes 524304 | tf_op jit(solution)/shard_map/psum | solution.py:61
  172.5 1.9 %copy.42 = f32[2048,64]{0,1:T(8,128)} copy(f32[2048,64]{0,1:T(8,128)} %all-reduce.2.cloned.1.call-done) | data formatting | bytes 1048576
  (43 shorter events, 8.7 us)
Async XLA Ops:
  6.5 67.3 %reduce-scatter.2.cloned.1.call-start = ((), (), s32[]{:S(2)}) async-start(), calls=%async_computation.1 | async-start | bytes 589824 | tf_op jit(solution)/shard_map/reduce_scatter | solution.py:37
  6.5 8.8 %collective-permute-start = (bf16[2048,64]{0,1:T(8,128)(2,1)}, bf16[2048,64]{0,1:T(8,128)(2,1)S(1)}, u32[]{:S(2)}, u32[]{:S(2)}) collective-permute-start(bf16[2048,64]{0,1:T(8,128)(2,1)} %param.7), channel_id=1, source_target_pairs={{0,1},{1,2},{2,3},{3,4},{4,5},{5,6},{6,7},{7,0},{8,9},{9,10},{10,1... | collective-permute-start | bytes 786440 | tf_op jit(solution)/shard_map/ppermute | solution.py:52
  15.3 25.2 %collective-permute-start.1 = (bf16[2048,64]{0,1:T(8,128)(2,1)S(1)}, bf16[2048,64]{0,1:T(8,128)(2,1)S(1)}, u32[]{:S(2)}, u32[]{:S(2)}) collective-permute-start(bf16[2048,64]{0,1:T(8,128)(2,1)S(1)} %collective-permute-done), channel_id=1, source_target_pairs={{0,1},{1,2},{2,3},{3,4},{4,5},{5,6},{6,7},{7,0},{8,9},{9,10},{10,1... | collective-permute-start | bytes 786440 | tf_op jit(solution)/shard_map/ppermute | solution.py:52
  15.5 4.4 %copy-start = (bf16[2048,64]{0,1:T(8,128)(2,1)S(1)}, bf16[2048,64]{0,1:T(8,128)(2,1)}, u32[]{:S(2)}) copy-start(bf16[2048,64]{0,1:T(8,128)(2,1)} %get-tuple-element.130) | copy-start | bytes 786436 | tf_op jit(solution)/shard_map/while
  21.6 4.5 %copy-start = (bf16[2048,64]{0,1:T(8,128)(2,1)S(1)}, bf16[2048,64]{0,1:T(8,128)(2,1)}, u32[]{:S(2)}) copy-start(bf16[2048,64]{0,1:T(8,128)(2,1)} %get-tuple-element.130) | copy-start | bytes 786436 | tf_op jit(solution)/shard_map/while
  27.7 4.4 %copy-start = (bf16[2048,64]{0,1:T(8,128)(2,1)S(1)}, bf16[2048,64]{0,1:T(8,128)(2,1)}, u32[]{:S(2)}) copy-start(bf16[2048,64]{0,1:T(8,128)(2,1)} %get-tuple-element.130) | copy-start | bytes 786436 | tf_op jit(solution)/shard_map/while
  33.8 4.4 %copy-start = (bf16[2048,64]{0,1:T(8,128)(2,1)S(1)}, bf16[2048,64]{0,1:T(8,128)(2,1)}, u32[]{:S(2)}) copy-start(bf16[2048,64]{0,1:T(8,128)(2,1)} %get-tuple-element.130) | copy-start | bytes 786436 | tf_op jit(solution)/shard_map/while
  40.5 70.1 %all-gather.2.cloned.1.call-start = ((), (), s32[]{:S(2)}) async-start(), calls=%async_computation.2 | async-start | bytes 1179648 | tf_op jit(solution)/shard_map/all_gather | solution.py:49
  40.5 7.7 %collective-permute-start.2 = (bf16[2048,64]{0,1:T(8,128)(2,1)S(1)}, bf16[2048,64]{0,1:T(8,128)(2,1)S(1)}, u32[]{:S(2)}, u32[]{:S(2)}) collective-permute-start(bf16[2048,64]{0,1:T(8,128)(2,1)S(1)} %collective-permute-done.1), channel_id=1, source_target_pairs={{0,1},{1,2},{2,3},{3,4},{4,5},{5,6},{6,7},{7,0},{8,9},{9,10},{10,1... | collective-permute-start | bytes 786440 | tf_op jit(solution)/shard_map/ppermute | solution.py:52
  48.2 8.3 %collective-permute-start.3 = (bf16[2048,64]{0,1:T(8,128)(2,1)S(1)}, bf16[2048,64]{0,1:T(8,128)(2,1)S(1)}, u32[]{:S(2)}, u32[]{:S(2)}) collective-permute-start(bf16[2048,64]{0,1:T(8,128)(2,1)S(1)} %collective-permute-done.2), channel_id=1, source_target_pairs={{0,1},{1,2},{2,3},{3,4},{4,5},{5,6},{6,7},{7,0},{8,9},{9,10},{10,1... | collective-permute-start | bytes 786440 | tf_op jit(solution)/shard_map/ppermute | solution.py:52
  56.5 8.1 %collective-permute-start.4 = (bf16[2048,64]{0,1:T(8,128)(2,1)S(1)}, bf16[2048,64]{0,1:T(8,128)(2,1)S(1)}, u32[]{:S(2)}, u32[]{:S(2)}) collective-permute-start(bf16[2048,64]{0,1:T(8,128)(2,1)S(1)} %collective-permute-done.3), channel_id=1, source_target_pairs={{0,1},{1,2},{2,3},{3,4},{4,5},{5,6},{6,7},{7,0},{8,9},{9,10},{10,1... | collective-permute-start | bytes 786440 | tf_op jit(solution)/shard_map/ppermute | solution.py:52
  64.6 25.2 %collective-permute-start.5 = (bf16[2048,64]{0,1:T(8,128)(2,1)S(1)}, bf16[2048,64]{0,1:T(8,128)(2,1)S(1)}, u32[]{:S(2)}, u32[]{:S(2)}) collective-permute-start(bf16[2048,64]{0,1:T(8,128)(2,1)S(1)} %collective-permute-done.4), channel_id=1, source_target_pairs={{0,1},{1,2},{2,3},{3,4},{4,5},{5,6},{6,7},{7,0},{8,9},{9,10},{10,1... | collective-permute-start | bytes 786440 | tf_op jit(solution)/shard_map/ppermute | solution.py:52
  64.6 107.9 %all-reduce.2.cloned.1.call-start = ((), (), s32[]{:S(2)}) async-start(), calls=%async_computation.3 | async-start | bytes 1048576 | tf_op jit(solution)/shard_map/psum | solution.py:61
  89.8 9.3 %collective-permute-start.6 = (bf16[2048,64]{0,1:T(8,128)(2,1)S(1)}, bf16[2048,64]{0,1:T(8,128)(2,1)S(1)}, u32[]{:S(2)}, u32[]{:S(2)}) collective-permute-start(bf16[2048,64]{0,1:T(8,128)(2,1)S(1)} %collective-permute-done.5), channel_id=1, source_target_pairs={{0,1},{1,2},{2,3},{3,4},{4,5},{5,6},{6,7},{7,0},{8,9},{9,10},{10,1... | collective-permute-start | bytes 786440 | tf_op jit(solution)/shard_map/ppermute | solution.py:52
  90.1 14.0 %copy-start.1 = (bf16[2048,64]{0,1:T(8,128)(2,1)S(1)}, bf16[2048,64]{0,1:T(8,128)(2,1)}, u32[]{:S(2)}) copy-start(bf16[2048,64]{0,1:T(8,128)(2,1)} %get-tuple-element.136) | copy-start | bytes 786436
  125.3 0.8 copy-start.2
Sparse Core Ops, SparseCore 0:
  40.6 33.1 reduce-scatter.1
  75.4 22.1 all-gather.1
  126.2 46.2 all-reduce.1
